TPU v7x, 32 devices: a whole 2x2x4 slice. The times are simulated.
32 devices in a mesh: dp: 4 (over y, x), fsdp: 8 (over z, core).
Axes of the slice: x: 2, y: 2, z: 4, core: 2. Of those that a mesh axis runs over, the one named last changes fastest.
Arguments:
- tokens: bfloat16 [32, 1024, 768], P(('dp', 'fsdp')), may hold values from -6 to 6
- lengths: int32 [32], P(('dp', 'fsdp')), may hold values from 256 to 1024, as said below
- cells: int32 [32, 1024], P(('dp', 'fsdp')), may hold values 0 or 1
- cotangent: bfloat16 [32, 1024, 768], P(('dp', 'fsdp')), may hold values from -6 to 6
- ln1_gain: bfloat16 [768], P('fsdp'), may hold values from 0.5 to 1.5
- ln1_bias: bfloat16 [768], P('fsdp'), may hold values from -3 to 3
- w_qkv: bfloat16 [768, 2304], P('fsdp'), may hold values from -0.21875 to 0.21875
- b_query: bfloat16 [768], P('fsdp'), may hold values from -6 to 6
- b_value: bfloat16 [768], P('fsdp'), may hold values from -6 to 6
- w_out: bfloat16 [768, 768], P('fsdp'), may hold values from -0.875 to 0.875
- b_out: bfloat16 [768], P('fsdp'), may hold values from -3 to 3
- ln2_gain: bfloat16 [768], P('fsdp'), may hold values from 0.5 to 1.5
- ln2_bias: bfloat16 [768], P('fsdp'), may hold values from -3 to 3
- w_up: bfloat16 [768, 3072], P('fsdp'), may hold values from -0.21875 to 0.21875
- b_up: bfloat16 [3072], P('fsdp'), may hold values from -3 to 3
- w_down: bfloat16 [3072, 768], P('fsdp'), may hold values from -0.109375 to 0.109375
- b_down: bfloat16 [768], P('fsdp'), may hold values from -3 to 3
Outputs:
- output: bfloat16 [32, 1024, 768], P(('dp', 'fsdp'))
- grad_tokens: float32 [32, 1024, 768], P(('dp', 'fsdp'))
- grad_ln1_gain: float32 [768], P('fsdp')
- grad_ln1_bias: float32 [768], P('fsdp')
- grad_w_qkv: float32 [768, 2304], P('fsdp')
- grad_b_query: float32 [768], P('fsdp')
- grad_b_value: float32 [768], P('fsdp')
- grad_w_out: float32 [768, 768], P('fsdp')
- grad_b_out: float32 [768], P('fsdp')
- grad_ln2_gain: float32 [768], P('fsdp')
- grad_ln2_bias: float32 [768], P('fsdp')
- grad_w_up: float32 [768, 3072], P('fsdp')
- grad_b_up: float32 [3072], P('fsdp')
- grad_w_down: float32 [3072, 768], P('fsdp')
- grad_b_down: float32 [768], P('fsdp')
Inputs may be any that keep to these rules, and one draw needn't show every extreme that they name: `lengths`: each sequence has at least 256 valid tokens, and some sequence fills all 1024 slots.
All inputs are finite; a program needn't handle non-finite values. No bound on the sum of `cells` on one device may be relied on, other than what follows from the above.
Results may differ from a plain program's by a relative error of at most 0.019.
Values may be sent and summed in bfloat16 or wider, within the bound.
A program may use at most 128 MiB of HBM per device.

v0:
```python
from functools import partial
import math
import jax
import jax.numpy as jnp
from jax import lax
from jax.sharding import PartitionSpec as P

H = 12
EPSILON = 1e-05
GELU_C = 0.7978845608028654
GELU_A = 0.044715


def norm_forward(values):
    row_mean = jnp.mean(values, axis=-1, keepdims=True)
    centered = values - row_mean
    inv_std = lax.rsqrt(jnp.mean(centered * centered, axis=-1, keepdims=True) + EPSILON)
    return (centered * inv_std, inv_std)


def norm_backward(grad_normed, normalized, inv_std, gain):
    scaled = grad_normed * gain
    return inv_std * (
        scaled
        - jnp.mean(scaled, axis=-1, keepdims=True)
        - normalized * jnp.mean(scaled * normalized, axis=-1, keepdims=True)
    )


def gelu_pair(values):
    cubic = values * values * values
    tanh_part = jnp.tanh(GELU_C * (values + GELU_A * cubic))
    result = 0.5 * values * (1.0 + tanh_part)
    slope = 0.5 * (1.0 + tanh_part) + 0.5 * values * (1.0 - tanh_part * tanh_part) * GELU_C * (
        1.0 + 3.0 * GELU_A * values * values
    )
    return (result, slope)


def allowed_blocks(lengths, cells, context):
    positions = jnp.arange(context)
    query_pos = positions[None, :, None]
    key_pos = positions[None, None, :]
    usable = (key_pos <= query_pos) & (key_pos < lengths[:, None, None]) & (cells[:, None, :] == 1)
    return usable | (key_pos == query_pos)


def split_heads(rows, seqs, context, heads):
    width = rows.shape[1]
    return rows.reshape(seqs, context, heads, width // heads).transpose(2, 0, 1, 3)


def join_heads(stacked):
    return stacked.transpose(1, 2, 0, 3).reshape(-1, stacked.shape[0] * stacked.shape[3])


def head_forward(allowed, operands):
    query_head, key_head, value_head = operands
    scores = jnp.einsum("sqd,skd->sqk", query_head, key_head, preferred_element_type=jnp.float32)
    scores = jnp.where(allowed, scores, -1e30)
    row_max = jnp.max(scores, axis=-1, keepdims=True)
    exponent = jnp.exp(scores - row_max)
    row_total = jnp.sum(exponent, axis=-1, keepdims=True)
    softmax_rows = (exponent / row_total).astype(jnp.bfloat16)
    attended = jnp.einsum(
        "sqk,skd->sqd", softmax_rows, value_head, preferred_element_type=jnp.float32
    )
    return (attended, (row_max + jnp.log(row_total))[..., 0])


def head_backward(allowed, operands):
    query_head, key_head, value_head, grad_head, log_total = operands
    scores = jnp.einsum("sqd,skd->sqk", query_head, key_head, preferred_element_type=jnp.float32)
    softmax_rows = jnp.where(allowed, jnp.exp(scores - log_total[..., None]), 0.0)
    grad_values = jnp.einsum(
        "sqk,sqd->skd",
        softmax_rows.astype(jnp.bfloat16),
        grad_head,
        preferred_element_type=jnp.float32,
    )
    grad_probs = jnp.einsum(
        "sqd,skd->sqk", grad_head, value_head, preferred_element_type=jnp.float32
    )
    inner = jnp.sum(softmax_rows * grad_probs, axis=-1, keepdims=True)
    grad_scores = (softmax_rows * (grad_probs - inner)).astype(jnp.bfloat16)
    grad_queries = jnp.einsum(
        "sqk,skd->sqd", grad_scores, key_head, preferred_element_type=jnp.float32
    )
    grad_keys = jnp.einsum(
        "sqk,sqd->skd", grad_scores, query_head, preferred_element_type=jnp.float32
    )
    return (grad_queries, grad_keys, grad_values)


def per_device(
    tokens,
    lengths,
    cells,
    cotangent,
    ln1_gain,
    ln1_bias,
    w_qkv,
    b_query,
    b_value,
    w_out,
    b_out,
    ln2_gain,
    ln2_bias,
    w_up,
    b_up,
    w_down,
    b_down,
):
    seqs, context, width = tokens.shape
    heads = H
    scale = 1.0 / math.sqrt(width // heads)
    attn_parts = (
        lax.all_gather(ln1_gain, "fsdp", axis=0, tiled=True),
        lax.all_gather(ln1_bias, "fsdp", axis=0, tiled=True),
        lax.all_gather(w_qkv, "fsdp", axis=0, tiled=True),
        lax.all_gather(b_query, "fsdp", axis=0, tiled=True),
        lax.all_gather(b_value, "fsdp", axis=0, tiled=True),
        lax.all_gather(w_out, "fsdp", axis=0, tiled=True),
        lax.all_gather(b_out, "fsdp", axis=0, tiled=True),
    )
    gain_one, shift_one, qkv_full, bias_query, bias_value, out_full, bias_out = attn_parts
    inputs = tokens.reshape(-1, width).astype(jnp.float32)
    normal_one, inv_one = norm_forward(inputs)
    normed_one = (normal_one * gain_one.astype(jnp.float32) + shift_one.astype(jnp.float32)).astype(
        jnp.bfloat16
    )
    projected = jnp.dot(normed_one, qkv_full, preferred_element_type=jnp.float32)
    queries = ((projected[:, :width] + bias_query.astype(jnp.float32)) * scale).astype(jnp.bfloat16)
    key_rows = projected[:, width : 2 * width].astype(jnp.bfloat16)
    value_rows = (projected[:, 2 * width :] + bias_value.astype(jnp.float32)).astype(jnp.bfloat16)
    allowed = allowed_blocks(lengths, cells, context)
    query_heads = split_heads(queries, seqs, context, heads)
    key_heads = split_heads(key_rows, seqs, context, heads)
    value_heads = split_heads(value_rows, seqs, context, heads)
    attended_heads, log_totals = lax.map(
        partial(head_forward, allowed), (query_heads, key_heads, value_heads)
    )
    attended = join_heads(attended_heads).astype(jnp.bfloat16)
    middle = (
        inputs
        + jnp.dot(attended, out_full, preferred_element_type=jnp.float32)
        + bias_out.astype(jnp.float32)
    )
    mlp_parts = (
        lax.all_gather(ln2_gain, "fsdp", axis=0, tiled=True),
        lax.all_gather(ln2_bias, "fsdp", axis=0, tiled=True),
        lax.all_gather(w_up, "fsdp", axis=0, tiled=True),
        lax.all_gather(b_up, "fsdp", axis=0, tiled=True),
        lax.all_gather(w_down, "fsdp", axis=0, tiled=True),
        lax.all_gather(b_down, "fsdp", axis=0, tiled=True),
    )
    gain_two, shift_two, up_full, bias_up, down_full, bias_down = mlp_parts
    normal_two, inv_two = norm_forward(middle)
    normed_two = (normal_two * gain_two.astype(jnp.float32) + shift_two.astype(jnp.float32)).astype(
        jnp.bfloat16
    )
    hidden_pre = jnp.dot(normed_two, up_full, preferred_element_type=jnp.float32) + bias_up.astype(
        jnp.float32
    )
    activated, slope = gelu_pair(hidden_pre)
    activated = activated.astype(jnp.bfloat16)
    mlp_out = jnp.dot(activated, down_full, preferred_element_type=jnp.float32) + bias_down.astype(
        jnp.float32
    )
    result = (middle + mlp_out).astype(jnp.bfloat16).reshape(tokens.shape)
    valid = (jnp.arange(context)[None, :] < lengths[:, None]).astype(jnp.float32).reshape(-1, 1)
    grad_out = cotangent.reshape(-1, width).astype(jnp.float32) * valid
    mlp_back = (
        lax.all_gather(ln2_gain, "fsdp", axis=0, tiled=True),
        lax.all_gather(ln2_bias, "fsdp", axis=0, tiled=True),
        lax.all_gather(w_up, "fsdp", axis=0, tiled=True),
        lax.all_gather(b_up, "fsdp", axis=0, tiled=True),
        lax.all_gather(w_down, "fsdp", axis=0, tiled=True),
        lax.all_gather(b_down, "fsdp", axis=0, tiled=True),
    )
    gain_two_back, unused_two, up_back, unused_up, down_back, unused_down = mlp_back
    grad_mlp = grad_out.astype(jnp.bfloat16)
    grad_down = jnp.einsum("rf,rd->fd", activated, grad_mlp, preferred_element_type=jnp.float32)
    grad_bias_down = jnp.sum(grad_mlp.astype(jnp.float32), axis=0)
    grad_act = jnp.einsum("rd,fd->rf", grad_mlp, down_back, preferred_element_type=jnp.float32)
    grad_hidden = (grad_act * slope).astype(jnp.bfloat16)
    grad_up = jnp.einsum("rd,rf->df", normed_two, grad_hidden, preferred_element_type=jnp.float32)
    grad_bias_up = jnp.sum(grad_hidden.astype(jnp.float32), axis=0)
    grad_normed_two = jnp.einsum(
        "rf,df->rd", grad_hidden, up_back, preferred_element_type=jnp.float32
    )
    grad_gain_two = jnp.sum(grad_normed_two * normal_two, axis=0)
    grad_shift_two = jnp.sum(grad_normed_two, axis=0)
    grad_middle = grad_out + norm_backward(
        grad_normed_two, normal_two, inv_two, gain_two_back.astype(jnp.float32)
    )
    mlp_rows = (
        lax.psum_scatter(
            grad_gain_two.astype(jnp.bfloat16), "fsdp", scatter_dimension=0, tiled=True
        ).astype(jnp.float32),
        lax.psum_scatter(
            grad_shift_two.astype(jnp.bfloat16), "fsdp", scatter_dimension=0, tiled=True
        ).astype(jnp.float32),
        lax.psum_scatter(
            grad_up.astype(jnp.bfloat16), "fsdp", scatter_dimension=0, tiled=True
        ).astype(jnp.float32),
        lax.psum_scatter(
            grad_bias_up.astype(jnp.bfloat16), "fsdp", scatter_dimension=0, tiled=True
        ).astype(jnp.float32),
        lax.psum_scatter(
            grad_down.astype(jnp.bfloat16), "fsdp", scatter_dimension=0, tiled=True
        ).astype(jnp.float32),
        lax.psum_scatter(
            grad_bias_down.astype(jnp.bfloat16), "fsdp", scatter_dimension=0, tiled=True
        ).astype(jnp.float32),
    )
    row_gain_two, row_shift_two, row_up, row_bias_up, row_down, row_bias_down = mlp_rows
    mlp_sums = (
        lax.psum(row_gain_two.astype(jnp.bfloat16), "dp").astype(jnp.float32),
        lax.psum(row_shift_two.astype(jnp.bfloat16), "dp").astype(jnp.float32),
        lax.psum(row_up.astype(jnp.bfloat16), "dp").astype(jnp.float32),
        lax.psum(row_bias_up.astype(jnp.bfloat16), "dp").astype(jnp.float32),
        lax.psum(row_down.astype(jnp.bfloat16), "dp").astype(jnp.float32),
        lax.psum(row_bias_down.astype(jnp.bfloat16), "dp").astype(jnp.float32),
    )
    attn_back = (
        lax.all_gather(ln1_gain, "fsdp", axis=0, tiled=True),
        lax.all_gather(ln1_bias, "fsdp", axis=0, tiled=True),
        lax.all_gather(w_qkv, "fsdp", axis=0, tiled=True),
        lax.all_gather(b_query, "fsdp", axis=0, tiled=True),
        lax.all_gather(b_value, "fsdp", axis=0, tiled=True),
        lax.all_gather(w_out, "fsdp", axis=0, tiled=True),
        lax.all_gather(b_out, "fsdp", axis=0, tiled=True),
    )
    gain_one_back, unused_shift, qkv_back, unused_query, unused_value, out_back, unused_out = (
        attn_back
    )
    grad_branch = grad_middle.astype(jnp.bfloat16)
    grad_out_proj = jnp.einsum(
        "rd,re->de", attended, grad_branch, preferred_element_type=jnp.float32
    )
    grad_bias_out = jnp.sum(grad_branch.astype(jnp.float32), axis=0)
    grad_attended = jnp.einsum(
        "re,de->rd", grad_branch, out_back, preferred_element_type=jnp.float32
    ).astype(jnp.bfloat16)
    grad_heads = split_heads(grad_attended, seqs, context, heads)
    grad_query_heads, grad_key_heads, grad_value_heads = lax.map(
        partial(head_backward, allowed),
        (query_heads, key_heads, value_heads, grad_heads, log_totals),
    )
    grad_queries = (join_heads(grad_query_heads) * scale).astype(jnp.bfloat16)
    grad_keys = join_heads(grad_key_heads).astype(jnp.bfloat16)
    grad_values = join_heads(grad_value_heads).astype(jnp.bfloat16)
    grad_projected = jnp.concatenate([grad_queries, grad_keys, grad_values], axis=1)
    grad_qkv = jnp.einsum(
        "rd,re->de", normed_one, grad_projected, preferred_element_type=jnp.float32
    )
    grad_bias_query = jnp.sum(grad_queries.astype(jnp.float32), axis=0)
    grad_bias_value = jnp.sum(grad_values.astype(jnp.float32), axis=0)
    grad_normed_one = jnp.einsum(
        "re,de->rd", grad_projected, qkv_back, preferred_element_type=jnp.float32
    )
    grad_gain_one = jnp.sum(grad_normed_one * normal_one, axis=0)
    grad_shift_one = jnp.sum(grad_normed_one, axis=0)
    grad_inputs = grad_middle + norm_backward(
        grad_normed_one, normal_one, inv_one, gain_one_back.astype(jnp.float32)
    )
    attn_rows = (
        lax.psum_scatter(
            grad_gain_one.astype(jnp.bfloat16), "fsdp", scatter_dimension=0, tiled=True
        ).astype(jnp.float32),
        lax.psum_scatter(
            grad_shift_one.astype(jnp.bfloat16), "fsdp", scatter_dimension=0, tiled=True
        ).astype(jnp.float32),
        lax.psum_scatter(
            grad_qkv.astype(jnp.bfloat16), "fsdp", scatter_dimension=0, tiled=True
        ).astype(jnp.float32),
        lax.psum_scatter(
            grad_bias_query.astype(jnp.bfloat16), "fsdp", scatter_dimension=0, tiled=True
        ).astype(jnp.float32),
        lax.psum_scatter(
            grad_bias_value.astype(jnp.bfloat16), "fsdp", scatter_dimension=0, tiled=True
        ).astype(jnp.float32),
        lax.psum_scatter(
            grad_out_proj.astype(jnp.bfloat16), "fsdp", scatter_dimension=0, tiled=True
        ).astype(jnp.float32),
        lax.psum_scatter(
            grad_bias_out.astype(jnp.bfloat16), "fsdp", scatter_dimension=0, tiled=True
        ).astype(jnp.float32),
    )
    row_gain_one, row_shift_one, row_qkv, row_query, row_value, row_out, row_bias_out = attn_rows
    attn_sums = (
        lax.psum(row_gain_one.astype(jnp.bfloat16), "dp").astype(jnp.float32),
        lax.psum(row_shift_one.astype(jnp.bfloat16), "dp").astype(jnp.float32),
        lax.psum(row_qkv.astype(jnp.bfloat16), "dp").astype(jnp.float32),
        lax.psum(row_query.astype(jnp.bfloat16), "dp").astype(jnp.float32),
        lax.psum(row_value.astype(jnp.bfloat16), "dp").astype(jnp.float32),
        lax.psum(row_out.astype(jnp.bfloat16), "dp").astype(jnp.float32),
        lax.psum(row_bias_out.astype(jnp.bfloat16), "dp").astype(jnp.float32),
    )
    return (
        result,
        grad_inputs.reshape(tokens.shape),
        attn_sums[0],
        attn_sums[1],
        attn_sums[2],
        attn_sums[3],
        attn_sums[4],
        attn_sums[5],
        attn_sums[6],
        mlp_sums[0],
        mlp_sums[1],
        mlp_sums[2],
        mlp_sums[3],
        mlp_sums[4],
        mlp_sums[5],
    )


def solution(mesh):
    in_specs = (
        P(("dp", "fsdp"), None, None),
        P(("dp", "fsdp")),
        P(("dp", "fsdp"), None),
        P(("dp", "fsdp"), None, None),
        P("fsdp"),
        P("fsdp"),
        P("fsdp", None),
        P("fsdp"),
        P("fsdp"),
        P("fsdp", None),
        P("fsdp"),
        P("fsdp"),
        P("fsdp"),
        P("fsdp", None),
        P("fsdp"),
        P("fsdp", None),
        P("fsdp"),
    )
    out_specs = (
        P(("dp", "fsdp"), None, None),
        P(("dp", "fsdp"), None, None),
        P("fsdp"),
        P("fsdp"),
        P("fsdp", None),
        P("fsdp"),
        P("fsdp"),
        P("fsdp", None),
        P("fsdp"),
        P("fsdp"),
        P("fsdp"),
        P("fsdp", None),
        P("fsdp"),
        P("fsdp", None),
        P("fsdp"),
    )
    return jax.shard_map(
        per_device, mesh=mesh, in_specs=in_specs, out_specs=out_specs, check_vma=False
    )
```

profile of v0, /device:TPU:0, one launch (start us, length us, event | category | flops | bytes accessed | tf_op | source)
XLA Modules:
  0.0 642.1 jit_solution(9640326640721068901)
XLA Ops:
  14.4 32.5 %all-reduce.18 = (bf16[768]{0:T(1024)(128)(2,1)S(1)}, bf16[768]{0:T(1024)(128)(2,1)S(1)}, bf16[768]{0:T(1024)(128)(2,1)S(1)}, bf16[768]{0:T(1024)(128)(2,1)S(1)}...) all-reduce(bf16[768]{0:T(1024)(128)(2,1)S(1)} %dynamic-update-slice, ...), channel_id=1, replica_groups=mesh['dp'=4,'fsdp'=8] {'fsdp'}, use_global_device_ids=true, to_apply=%add.1 | all-reduce | flops 5376 | bytes 21504
  52.8 12.7 %all-gather = bf16[8,1,384]{2,1,0:T(2,128)(2,1)S(1)} all-gather(bf16[1,1,384]{2,1,0:T(2,128)(2,1)S(1)} %reshape.386), channel_id=1, replica_groups=mesh['dp'=4,'fsdp'=8] {'fsdp'}, dimensions={0}, use_global_device_ids=true | all-gather | bytes 6912 | tf_op jit(solution)/shard_map/all_gather | solution.py:153
  65.7 6.3 fusion.98
  87.1 69.4 %while.30 = (s32[]{:T(128)}, bf16[12,1,1024,64]{2,3,1,0:T(8,128)(2,1)S(1)}, f32[12,1,1024]{2,1,0:T(1,128)S(1)}, bf16[12,1,1024,64]{3,2,1,0:T(8,128)(2,1)}, bf16[...) while((s32[]{:T(128)}, ...), condition=%wide.region_5.6_spmd.clone.clone, body=%wide.region_2.5_spmd.clone.sunk.clone | while | flops 281017344 | bytes 13676633 | solution.py:140
  157.7 3.9 fusion.106
  162.0 10.7 %fusion.100 = f32[1024,3072]{1,0:T(8,128)} fusion(bf16[768,3072]{1,0:T(8,128)(2,1)} %all-gather.10.cloned.1.call-done, f32[1024,768]{0,1:T(8,128)S(1)} %get-tuple-element.332, f32[768]{0:T(1024)S(1)} %convert_element_type.246, f32[768]{0:T(1024)S(1)} %convert_element_type.245, f32[1024]{0:T(1024)S(1)} %add_rsqrt_fusion, f32[1024]{0:T(1024)S(1)} %broadcast_multiply_fusion.4), kind=kOutput, calls=%fused_computation.139 | convolution fusion | flops 4835770368 | bytes 20461568 | tf_op jit(solution)/shard_map/dot_general | solution.py:162
  172.6 9.1 %all-gather.12.cloned.1.call-done = bf16[3072,768]{1,0:T(8,128)(2,1)} async-done(((bf16[384,768]{1,0:T(8,128)(2,1)}), bf16[3072,768]{1,0:T(8,128)(2,1)}) %all-gather.12.cloned.1.call-update) | async-done | bytes 4718608 | tf_op jit(solution)/shard_map/all_gather | solution.py:154
  181.7 16.5 %fusion.109 = (bf16[3072]{0:T(1024)(128)(2,1)S(1)}, bf16[1024,3072]{1,0:T(8,128)(2,1)S(1)}) fusion(f32[1024,3072]{1,0:T(8,128)} %fusion.100, f32[3072]{0:T(1024)S(1)} %bitcast.226, bf16[3072,768]{1,0:T(8,128)(2,1)} %all-gather.12.cloned.1.call-done, bf16[1,1024,768]{1,2,0:T(8,128)(2,1)} %copy.72, f32[1024]{0:T(1024)S(1)} %fusion.92), kind=kOutput, calls=%fused_computation.147 | convolution fusion | flops 4900254720 | bytes 25188352 | tf_op jit(solution)/shard_map/rd,fd->rf/dot_general | solution.py:185
  198.3 6.7 %fusion.108 = (bf16[768]{0:T(1024)(128)(2,1)S(1)}, f32[1024,768]{1,0:T(8,128)}) fusion(bf16[1024,3072]{1,0:T(8,128)(2,1)S(1)} %get-tuple-element.338, bf16[768,3072]{1,0:T(8,128)(2,1)S(1)} %copy-done.12), kind=kOutput, calls=%fused_computation.146 | convolution fusion | flops 4832623616 | bytes 14157312 | tf_op jit(solution)/shard_map/rf,df->rd/dot_general | solution.py:189
  217.8 4.8 convolution_convert_fusion.3
  222.6 4.3 copy.74
  226.9 171.0 %while.31 = (s32[]{:T(128)}, f32[12,1,1024,64]{2,3,1,0:T(8,128)}, bf16[12,1,1024,64]{2,3,1,0:T(8,128)(2,1)}, bf16[12,1,1024,64]{2,3,1,0:T(8,128)(2,1)}, bf16[12,...) while((s32[]{:T(128)}, f32[12,1,1024,64]{2,3,1,0:T(8,128)}, ...), condition=%wide.region_12.13_spmd.clone.clone, body=%wide.region_10.12_spmd.clone.sunk.clone | while | flops 684719104 | bytes 46689448 | solution.py:247
  228.6 3.8 multiply_reduce_fusion.8
  242.9 3.8 multiply_reduce_fusion.8
  401.5 7.3 %convolution_convert_fusion.2 = bf16[768,2304]{1,0:T(8,128)(2,1)} fusion(bf16[1024,768]{0,1:T(8,128)(2,1)} %bitcast.24, bf16[1024,768]{0,1:T(8,128)(2,1)S(1)} %bitcast.214, bf16[1024,768]{0,1:T(8,128)(2,1)S(1)} %bitcast.221, bf16[1,1024,768]{1,2,0:T(8,128)(2,1)S(1)} %copy-done.1, f32[768]{0:T(1024)S(1)} %copy-done.24, f32[768]{0:T(1024)S(1)} %copy-done.19, ...), kind=kOutput, calls=%fused_computation.77 | convolution fusion | flops 3644522496 | bytes 9844736 | tf_op jit(solution)/shard_map/rd,re->de/dot_general | solution.py:255
  408.8 9.7 %convolution_convert_fusion.1 = bf16[768,3072]{1,0:T(8,128)(2,1)} fusion(bf16[1024,3072]{1,0:T(8,128)(2,1)} %copy-done.35, f32[1024,768]{0,1:T(8,128)S(1)} %get-tuple-element.332, f32[768]{0:T(1024)S(1)} %convert_element_type.246, f32[768]{0:T(1024)S(1)} %convert_element_type.245, f32[1024]{0:T(1024)S(1)} %add_rsqrt_fusion, ...), kind=kOutput, calls=%fused_computation.76 | convolution fusion | flops 4838129664 | bytes 14170112 | tf_op jit(solution)/shard_map/rd,rf->df/dot_general | solution.py:187
  418.6 13.9 %convolution_convert_fusion = bf16[3072,768]{1,0:T(8,128)(2,1)} fusion(bf16[1,1024,768]{1,2,0:T(8,128)(2,1)} %copy.72, f32[1024]{0:T(1024)S(1)} %fusion.92, f32[1024,3072]{1,0:T(8,128)} %fusion.100, f32[3072]{0:T(1024)S(1)} %bitcast.227), kind=kOutput, calls=%fused_computation.75 | convolution fusion | flops 4868014080 | bytes 18890752 | tf_op jit(solution)/shard_map/rf,rd->fd/dot_general | solution.py:183
  434.1 9.1 %fusion.107 = (bf16[768]{0:T(1024)(128)(2,1)S(1)}, f32[1024,768]{1,0:T(8,128)}) fusion(bf16[768,2304]{1,0:T(8,128)(2,1)} %all-gather.6.cloned.1.call-done, bf16[1024,768]{0,1:T(8,128)(2,1)} %bitcast.24, bf16[1024,768]{0,1:T(8,128)(2,1)} %bitcast.213, bf16[1024,768]{0,1:T(8,128)(2,1)} %bitcast.222), kind=kOutput, calls=%fused_computation.145 | convolution fusion | flops 3638820096 | bytes 11404800 | tf_op jit(solution)/shard_map/re,de->rd/dot_general | solution.py:260
  452.1 28.3 %all-reduce.17 = (bf16[768]{0:T(1024)(128)(2,1)S(1)}, bf16[768]{0:T(1024)(128)(2,1)S(1)}, bf16[768]{0:T(1024)(128)(2,1)S(1)}, bf16[768]{0:T(1024)(128)(2,1)S(1)}...) all-reduce(bf16[768]{0:T(1024)(128)(2,1)S(1)} %dynamic-update-slice, ...), channel_id=1, replica_groups=mesh['dp'=4,'fsdp'=8] {'fsdp'}, use_global_device_ids=true, to_apply=%add.7 | all-reduce | flops 9984 | bytes 39936
  481.1 10.0 %all-reduce.19 = (bf16[96]{0:T(256)(128)(2,1)S(1)}, bf16[96]{0:T(256)(128)(2,1)S(1)}, bf16[96]{0:T(256)(128)(2,1)S(1)}, bf16[96]{0:T(256)(128)(2,1)S(1)}, bf16[9...) all-reduce(bf16[96]{0:T(256)(128)(2,1)S(1)} %dynamic-slice.9, ...), channel_id=1, replica_groups=mesh['dp'=4,'fsdp'=8] {'dp'}, use_global_device_ids=true, to_apply=%region_17.18 | all-reduce | flops 1152 | bytes 4608 | tf_op jit(solution)/shard_map/psum | solution.py:293
  495.7 6.0 fusion.78
  507.6 55.4 %reduce-scatter.11.cloned.1.call-done = bf16[384,768]{1,0:T(8,128)(2,1)} async-done(((bf16[3072,768]{1,0:T(8,128)(2,1)}), bf16[384,768]{1,0:T(8,128)(2,1)}) %reduce-scatter.11.cloned.1.call-update) | async-done | bytes 589840 | tf_op jit(solution)/shard_map/reduce_scatter | solution.py:210
  562.9 11.6 %fusion.88 = bf16[1,1024,768]{1,2,0:T(8,128)(2,1)} fusion(f32[1024,768]{0,1:T(8,128)S(1)} %get-tuple-element.332, f32[768]{0:T(1024)S(1)} %convert_element_type.250, bf16[3072,768]{1,0:T(8,128)(2,1)} %all-gather.12.cloned.1.call-done, f32[1024,3072]{1,0:T(8,128)} %fusion.100, f32[3072]{0:T(1024)S(1)} %bitcast.228), kind=kOutput, calls=%fused_computation.120 | convolution fusion | flops 4865654784 | bytes 22035456 | tf_op jit(solution)/shard_map/dot_general | solution.py:167
  577.1 51.9 %all-reduce.23.cloned.1.call-done = (bf16[96,2304]{1,0:T(8,128)(2,1)}, bf16[96,768]{1,0:T(8,128)(2,1)}, bf16[96,3072]{1,0:T(8,128)(2,1)}, bf16[384,768]{1,0:T(8,128)(2,1)}) async-done(((bf16[96,2304]{1,0:T(8,128)(2,1)}, bf16[96,768]{1,0:T(8,128)(2,1)}, bf16[96,3072]{1,0:T(8,128)(2,1)}, bf16[384,768]{1,0:T(8,128)(2,1)}), (bf16[96,2304]{1,0:T(8,128)(2,1)}, bf16[96,768]{1,0:T(8,128)(2,1)}, ...) | async-done | bytes 1769488 | tf_op jit(solution)/shard_map/psum | solution.py:295
  (370 shorter events, 305.7 us)
Async XLA Ops:
  7.2 58.5 %all-gather.6.cloned.1.call-start = ((), (), s32[]{:S(2)}) async-start(), calls=%async_computation.4 | async-start | bytes 3981312 | tf_op jit(solution)/shard_map/all_gather | solution.py:120
  7.9 148.7 %all-gather.8.cloned.1.call-start = ((), (), s32[]{:S(2)}) async-start(), calls=%async_computation.5 | async-start | bytes 1327104 | tf_op jit(solution)/shard_map/all_gather | solution.py:123
  8.7 153.3 %all-gather.10.cloned.1.call-start = ((), (), s32[]{:S(2)}) async-start(), calls=%async_computation.6 | async-start | bytes 5308416 | tf_op jit(solution)/shard_map/all_gather | solution.py:152
  9.4 172.3 %all-gather.12.cloned.1.call-start = ((), (), s32[]{:S(2)}) async-start(), calls=%async_computation.7 | async-start | bytes 5308416 | tf_op jit(solution)/shard_map/all_gather | solution.py:154
  10.0 495.4 %reduce-scatter.7.cloned.1.call-start = ((), (), s32[]{:S(2)}) async-start(), calls=%async_computation.9 | async-start | bytes 1327104 | tf_op jit(solution)/shard_map/reduce_scatter | solution.py:284
  10.2 61.7 %copy-start.3 = (bf16[12,1,1024,64]{2,3,1,0:T(8,128)(2,1)}, bf16[12,1,1024,64]{2,3,1,0:T(8,128)(2,1)S(1)}, u32[]{:S(2)}) copy-start(bf16[12,1,1024,64]{2,3,1,0:T(8,128)(2,1)S(1)} %fusion.104) | copy-start | bytes 4718596
  10.3 3.6 copy-start.32
  10.3 3.9 copy-start.33
  46.9 18.7 %copy-start.18 = (f32[768]{0:T(1024)}, f32[768]{0:T(1024)S(1)}, u32[]{:S(2)}) copy-start(f32[768]{0:T(1024)S(1)} %convert_element_type.234) | copy-start | bytes 9220
  46.9 18.8 %copy-start.23 = (f32[768]{0:T(1024)}, f32[768]{0:T(1024)S(1)}, u32[]{:S(2)}) copy-start(f32[768]{0:T(1024)S(1)} %convert_element_type.235) | copy-start | bytes 9220
  48.6 17.0 %copy-start = (bf16[1,1024,768]{1,2,0:T(8,128)(2,1)}, bf16[1,1024,768]{1,2,0:T(8,128)(2,1)S(1)}, u32[]{:S(2)}) copy-start(bf16[1,1024,768]{1,2,0:T(8,128)(2,1)S(1)} %copy.64) | copy-start | bytes 4718596
  48.6 4.2 copy-start.26
  48.9 23.0 %copy-start.16 = (f32[1024]{0:T(1024)}, f32[1024]{0:T(1024)S(1)}, u32[]{:S(2)}) copy-start(f32[1024]{0:T(1024)S(1)} %broadcast_multiply_fusion.5) | copy-start | bytes 12292
  49.4 22.6 %copy-start.20 = (f32[1024]{0:T(1024)}, f32[1024]{0:T(1024)S(1)}, u32[]{:S(2)}) copy-start(f32[1024]{0:T(1024)S(1)} %add_rsqrt_fusion.1) | copy-start | bytes 12292
  181.7 16.5 %copy-start.12 = (bf16[768,3072]{1,0:T(8,128)(2,1)S(1)}, bf16[768,3072]{1,0:T(8,128)(2,1)}, u32[]{:S(2)}) copy-start(bf16[768,3072]{1,0:T(8,128)(2,1)} %all-gather.10.cloned.1.call-done) | copy-start | bytes 14155780
  198.3 6.8 %copy-start.35 = (bf16[1024,3072]{1,0:T(8,128)(2,1)}, bf16[1024,3072]{1,0:T(8,128)(2,1)S(1)}, u32[]{:S(2)}) copy-start(bf16[1024,3072]{1,0:T(8,128)(2,1)S(1)} %get-tuple-element.338) | copy-start | bytes 18874372
  217.7 287.6 %reduce-scatter.5.cloned.1.call-start = ((), (), s32[]{:S(2)}) async-start(), calls=%async_computation.8 | async-start | bytes 3981312 | tf_op jit(solution)/shard_map/reduce_scatter | solution.py:275
  397.8 3.6 copy-start.17
  397.8 3.6 copy-start.19
  408.8 98.8 %reduce-scatter.9.cloned.1.call-start = ((), (), s32[]{:S(2)}) async-start(), calls=%async_computation.10 | async-start | bytes 5308416 | tf_op jit(solution)/shard_map/reduce_scatter | solution.py:204
  418.6 144.3 %reduce-scatter.11.cloned.1.call-start = ((), (), s32[]{:S(2)}) async-start(), calls=%async_computation.11 | async-start | bytes 5308416 | tf_op jit(solution)/shard_map/reduce_scatter | solution.py:210
  432.5 196.5 %all-reduce.23.cloned.1.call-start = ((), (), s32[]{:S(2)}) async-start(), calls=%async_computation.12 | async-start | bytes 3538944 | tf_op jit(solution)/shard_map/psum | solution.py:295
  629.0 4.4 copy-start.14
  629.0 5.4 copy-start.15
  (43 other events, 93.2 us)
Sparse Core Ops, SparseCore 0:
  9.6 44.6 all-gather.5
  56.0 21.6 all-gather.7
  79.3 50.8 all-gather.9
  131.7 49.9 all-gather.11
  217.8 31.6 reduce-scatter.6
  408.9 42.4 reduce-scatter.4
  453.7 53.8 reduce-scatter.8
  509.9 53.0 reduce-scatter.10
  566.4 62.6 all-reduce.22
where the time goes:
time: 652 us; the launch traced here: 642 us
  matrix products  307 us (47%)
  waiting for transfers between devices  121 us (19%)
  blocking collectives  83.5 us (13%)
  local copies, waits for them, and re-layouts  57.5 us (9%)
  other arithmetic  54 us (8%)
  between operations  17.4 us (3%)
    unnamed x2, blocking collectives  60.8 us
    reduce_scatter x1, waiting for transfers between devices, per_device(): lax.psum_scatter(grad_down.astype(jnp.bfloat16), 'fsdp', scatter_dimensio...  55.4 us
    psum x1, waiting for transfers between devices, per_device(): lax.psum(row_qkv.astype(jnp.bfloat16), 'dp').astype(jnp.float32)  51.9 us
    dot_general x12, matrix products, head_backward(): jnp.einsum('sqd,skd->sqk', query_head, key_head, preferred_element_type=j...  45.3 us
    dot_general x12, matrix products, head_forward(): jnp.einsum('sqd,skd->sqk', query_head, key_head, preferred_element_type=j...  39.4 us
    dot_general x12, matrix products, head_backward(): jnp.einsum('sqk,sqd->skd', softmax_rows.astype(jnp.bfloat16), grad_head,...  28.5 us
    dot_general x12, matrix products, head_backward(): jnp.einsum('sqk,skd->sqd', grad_scores, key_head, preferred_element_type=...  27.8 us
    unnamed x103, local copies, waits for them, and re-layouts  27.4 us
  transfers between devices with their start and end apart: 9, of which 4 were waited for; matrix products, arithmetic and copies ran while one was open for 56% of the time, Pallas kernels for 0%

commit v1 on v0

--- a/solution.py
+++ b/solution.py
@@ -292,7 +292,7 @@
     attn_sums = (
         lax.psum(row_gain_one.astype(jnp.bfloat16), "dp").astype(jnp.float32),
         lax.psum(row_shift_one.astype(jnp.bfloat16), "dp").astype(jnp.float32),
-        lax.psum(row_qkv.astype(jnp.bfloat16), "dp").astype(jnp.float32),
+        jnp.sum(lax.all_gather(row_qkv.astype(jnp.bfloat16), "dp"), axis=0).astype(jnp.float32),
         lax.psum(row_query.astype(jnp.bfloat16), "dp").astype(jnp.float32),
         lax.psum(row_value.astype(jnp.bfloat16), "dp").astype(jnp.float32),
         lax.psum(row_out.astype(jnp.bfloat16), "dp").astype(jnp.float32),

time: 652 us -> 706 us (1.083)
  waiting for transfers between devices: 121 us -> 179 us
    reduce_scatter x1, waiting for transfers between devices: 2.21 us -> 43.2 us  [per_device(): lax.psum_scatter(grad_up.astype(jnp.bfloat16), 'fsdp', scatter_dimension=...]
    reduce_scatter x1, waiting for transfers between devices: 0.01 us -> 14.1 us  [per_device(): lax.psum_scatter(grad_qkv.astype(jnp.bfloat16), 'fsdp', scatter_dimension...]
    unnamed x103 -> x101, local copies, waits for them, and re-layouts: 27.4 us -> 24.7 us
  transfers between devices with their start and end apart: 9 -> 10, of which waited for: 4 -> 5; matrix products, arithmetic and copies ran while one was open for 56% -> 27% of each run, Pallas kernels for 0% -> 0%
where the time goes in v1:
time: 706 us; the launch traced here: 696 us
  matrix products  307 us (43%)
  waiting for transfers between devices  179 us (25%)
  blocking collectives  82.4 us (12%)
  local copies, waits for them, and re-layouts  54.7 us (8%)
  other arithmetic  53.9 us (8%)
  between operations  17.9 us (3%)
    unnamed x2, blocking collectives  59.4 us
    reduce_scatter x1, waiting for transfers between devices, per_device(): lax.psum_scatter(grad_down.astype(jnp.bfloat16), 'fsdp', scatter_dimensio...  55.4 us
    psum x1, waiting for transfers between devices, per_device(): lax.psum(row_out.astype(jnp.bfloat16), 'dp').astype(jnp.float32)  54.1 us
    dot_general x12, matrix products, head_backward(): jnp.einsum('sqd,skd->sqk', query_head, key_head, preferred_element_type=j...  45.3 us
    reduce_scatter x1, waiting for transfers between devices, per_device(): lax.psum_scatter(grad_up.astype(jnp.bfloat16), 'fsdp', scatter_dimension=...  43.2 us
    dot_general x12, matrix products, head_forward(): jnp.einsum('sqd,skd->sqk', query_head, key_head, preferred_element_type=j...  39.5 us
    dot_general x12, matrix products, head_backward(): jnp.einsum('sqk,sqd->skd', softmax_rows.astype(jnp.bfloat16), grad_head,...  28.5 us
    dot_general x12, matrix products, head_backward(): jnp.einsum('sqk,skd->sqd', grad_scores, key_head, preferred_element_type=...  27.8 us
  transfers between devices with their start and end apart: 10, of which 5 were waited for; matrix products, arithmetic and copies ran while one was open for 27% of the time, Pallas kernels for 0%

profile of v1, /device:TPU:0, one launch (start us, length us, event | category | flops | bytes accessed | tf_op | source)
XLA Modules:
  0.0 696.0 jit_solution(16230542805820119457)
XLA Ops:
  14.4 32.5 %all-reduce.18 = (bf16[768]{0:T(1024)(128)(2,1)S(1)}, bf16[768]{0:T(1024)(128)(2,1)S(1)}, bf16[768]{0:T(1024)(128)(2,1)S(1)}, bf16[768]{0:T(1024)(128)(2,1)S(1)}...) all-reduce(bf16[768]{0:T(1024)(128)(2,1)S(1)} %dynamic-update-slice, ...), channel_id=1, replica_groups=mesh['dp'=4,'fsdp'=8] {'fsdp'}, use_global_device_ids=true, to_apply=%add.1 | all-reduce | flops 5376 | bytes 21504
  52.8 12.7 %all-gather.1 = bf16[8,1,384]{2,1,0:T(2,128)(2,1)S(1)} all-gather(bf16[1,1,384]{2,1,0:T(2,128)(2,1)S(1)} %reshape.387), channel_id=1, replica_groups=mesh['dp'=4,'fsdp'=8] {'fsdp'}, dimensions={0}, use_global_device_ids=true | all-gather | bytes 6912 | tf_op jit(solution)/shard_map/all_gather | solution.py:153
  65.6 6.3 fusion.98
  87.1 69.5 %while.30 = (s32[]{:T(128)}, bf16[12,1,1024,64]{2,3,1,0:T(8,128)(2,1)S(1)}, f32[12,1,1024]{2,1,0:T(1,128)S(1)}, bf16[12,1,1024,64]{3,2,1,0:T(8,128)(2,1)}, bf16[...) while((s32[]{:T(128)}, ...), condition=%wide.region_5.6_spmd.clone.clone, body=%wide.region_2.5_spmd.clone.sunk.clone | while | flops 281017344 | bytes 13676633 | solution.py:140
  157.7 3.9 fusion.106
  162.0 10.7 %fusion.100 = f32[1024,3072]{1,0:T(8,128)} fusion(bf16[768,3072]{1,0:T(8,128)(2,1)} %all-gather.12.cloned.1.call-done, f32[1024,768]{0,1:T(8,128)S(1)} %get-tuple-element.331, f32[768]{0:T(1024)S(1)} %convert_element_type.248, f32[768]{0:T(1024)S(1)} %convert_element_type.247, f32[1024]{0:T(1024)S(1)} %add_rsqrt_fusion, f32[1024]{0:T(1024)S(1)} %broadcast_multiply_fusion.4), kind=kOutput, calls=%fused_computation.139 | convolution fusion | flops 4835770368 | bytes 20461568 | tf_op jit(solution)/shard_map/dot_general | solution.py:162
  172.7 9.0 %all-gather.14.cloned.1.call-done = bf16[3072,768]{1,0:T(8,128)(2,1)} async-done(((bf16[384,768]{1,0:T(8,128)(2,1)}), bf16[3072,768]{1,0:T(8,128)(2,1)}) %all-gather.14.cloned.1.call-update) | async-done | bytes 4718608 | tf_op jit(solution)/shard_map/all_gather | solution.py:154
  181.7 16.5 %fusion.109 = (bf16[3072]{0:T(1024)(128)(2,1)S(1)}, bf16[1024,3072]{1,0:T(8,128)(2,1)S(1)}) fusion(f32[1024,3072]{1,0:T(8,128)} %fusion.100, f32[3072]{0:T(1024)S(1)} %bitcast.228, bf16[3072,768]{1,0:T(8,128)(2,1)} %all-gather.14.cloned.1.call-done, bf16[1,1024,768]{1,2,0:T(8,128)(2,1)} %copy.72, f32[1024]{0:T(1024)S(1)} %fusion.92), kind=kOutput, calls=%fused_computation.147 | convolution fusion | flops 4900254720 | bytes 25188352 | tf_op jit(solution)/shard_map/rd,fd->rf/dot_general | solution.py:185
  198.2 6.8 fusion.108
  216.3 4.1 copy.74
  220.4 171.1 %while.31 = (s32[]{:T(128)}, f32[12,1,1024,64]{2,3,1,0:T(8,128)}, bf16[12,1,1024,64]{2,3,1,0:T(8,128)(2,1)}, bf16[12,1,1024,64]{2,3,1,0:T(8,128)(2,1)}, bf16[12,...) while((s32[]{:T(128)}, f32[12,1,1024,64]{2,3,1,0:T(8,128)}, ...), condition=%wide.region_12.13_spmd.clone.clone, body=%wide.region_10.12_spmd.clone.sunk.clone | while | flops 684719104 | bytes 46689448 | solution.py:247
  395.2 7.3 %convolution_convert_fusion.2 = bf16[768,2304]{1,0:T(8,128)(2,1)} fusion(bf16[1024,768]{0,1:T(8,128)(2,1)} %bitcast.24, bf16[1024,768]{0,1:T(8,128)(2,1)S(1)} %bitcast.215, bf16[1024,768]{0,1:T(8,128)(2,1)S(1)} %bitcast.223, bf16[1,1024,768]{1,2,0:T(8,128)(2,1)S(1)} %copy-done.1, f32[768]{0:T(1024)S(1)} %copy-done.22, f32[768]{0:T(1024)S(1)} %copy-done.17, ...), kind=kOutput, calls=%fused_computation.77 | convolution fusion | flops 3644522496 | bytes 9844736 | tf_op jit(solution)/shard_map/rd,re->de/dot_general | solution.py:255
  402.6 4.8 convolution_convert_fusion.4
  407.4 9.8 %convolution_convert_fusion.1 = bf16[768,3072]{1,0:T(8,128)(2,1)} fusion(bf16[1024,3072]{1,0:T(8,128)(2,1)} %copy-done.34, f32[1024,768]{0,1:T(8,128)S(1)} %get-tuple-element.331, f32[768]{0:T(1024)S(1)} %convert_element_type.248, f32[768]{0:T(1024)S(1)} %convert_element_type.247, f32[1024]{0:T(1024)S(1)} %add_rsqrt_fusion, ...), kind=kOutput, calls=%fused_computation.76 | convolution fusion | flops 4838129664 | bytes 14170112 | tf_op jit(solution)/shard_map/rd,rf->df/dot_general | solution.py:187
  417.3 13.7 %convolution_convert_fusion = bf16[3072,768]{1,0:T(8,128)(2,1)} fusion(bf16[1,1024,768]{1,2,0:T(8,128)(2,1)} %copy.72, f32[1024]{0:T(1024)S(1)} %fusion.92, f32[1024,3072]{1,0:T(8,128)} %fusion.100, f32[3072]{0:T(1024)S(1)} %bitcast.229), kind=kOutput, calls=%fused_computation.75 | convolution fusion | flops 4868014080 | bytes 18890752 | tf_op jit(solution)/shard_map/rf,rd->fd/dot_general | solution.py:183
  431.0 14.1 %reduce-scatter.5.cloned.1.call-done = bf16[96,2304]{1,0:T(8,128)(2,1)} async-done(((bf16[768,2304]{1,0:T(8,128)(2,1)}), bf16[96,2304]{1,0:T(8,128)(2,1)}) %reduce-scatter.5.cloned.1.call-update) | async-done | bytes 442384 | tf_op jit(solution)/shard_map/reduce_scatter | solution.py:275
  447.0 9.0 %fusion.107 = (bf16[768]{0:T(1024)(128)(2,1)S(1)}, f32[1024,768]{1,0:T(8,128)}) fusion(bf16[768,2304]{1,0:T(8,128)(2,1)} %all-gather.8.cloned.1.call-done, bf16[1024,768]{0,1:T(8,128)(2,1)} %bitcast.24, bf16[1024,768]{0,1:T(8,128)(2,1)} %bitcast.214, bf16[1024,768]{0,1:T(8,128)(2,1)} %bitcast.224), kind=kOutput, calls=%fused_computation.145 | convolution fusion | flops 3638820096 | bytes 11404800 | tf_op jit(solution)/shard_map/re,de->rd/dot_general | solution.py:260
  464.8 26.9 %all-reduce.17 = (bf16[768]{0:T(1024)(128)(2,1)S(1)}, bf16[768]{0:T(1024)(128)(2,1)S(1)}, bf16[768]{0:T(1024)(128)(2,1)S(1)}, bf16[768]{0:T(1024)(128)(2,1)S(1)}...) all-reduce(bf16[768]{0:T(1024)(128)(2,1)S(1)} %dynamic-update-slice, ...), channel_id=1, replica_groups=mesh['dp'=4,'fsdp'=8] {'fsdp'}, use_global_device_ids=true, to_apply=%add.7 | all-reduce | flops 9984 | bytes 39936
  491.7 43.2 %reduce-scatter.9.cloned.1.call-done = bf16[96,3072]{1,0:T(8,128)(2,1)} async-done(((bf16[768,3072]{1,0:T(8,128)(2,1)}), bf16[96,3072]{1,0:T(8,128)(2,1)}) %reduce-scatter.9.cloned.1.call-update) | async-done | bytes 589840 | tf_op jit(solution)/shard_map/reduce_scatter | solution.py:204
  534.9 55.4 %reduce-scatter.11.cloned.1.call-done = bf16[384,768]{1,0:T(8,128)(2,1)} async-done(((bf16[3072,768]{1,0:T(8,128)(2,1)}), bf16[384,768]{1,0:T(8,128)(2,1)}) %reduce-scatter.11.cloned.1.call-update) | async-done | bytes 589840 | tf_op jit(solution)/shard_map/reduce_scatter | solution.py:210
  590.3 11.6 %fusion.88 = bf16[1,1024,768]{1,2,0:T(8,128)(2,1)} fusion(f32[1024,768]{0,1:T(8,128)S(1)} %get-tuple-element.331, f32[768]{0:T(1024)S(1)} %convert_element_type.252, bf16[3072,768]{1,0:T(8,128)(2,1)} %all-gather.14.cloned.1.call-done, f32[1024,3072]{1,0:T(8,128)} %fusion.100, f32[3072]{0:T(1024)S(1)} %bitcast.230), kind=kOutput, calls=%fused_computation.120 | convolution fusion | flops 4865654784 | bytes 22035456 | tf_op jit(solution)/shard_map/dot_general | solution.py:167
  602.5 10.2 %all-reduce.19 = (bf16[96]{0:T(256)(128)(2,1)S(1)}, bf16[96]{0:T(256)(128)(2,1)S(1)}, bf16[96]{0:T(256)(128)(2,1)S(1)}, bf16[96]{0:T(256)(128)(2,1)S(1)}, bf16[9...) all-reduce(bf16[96]{0:T(256)(128)(2,1)S(1)} %dynamic-slice.9, ...), channel_id=1, replica_groups=mesh['dp'=4,'fsdp'=8] {'dp'}, use_global_device_ids=true, to_apply=%region_17.18 | all-reduce | flops 1152 | bytes 4608 | tf_op jit(solution)/shard_map/psum | solution.py:293
  617.5 4.3 fusion.78
  629.4 54.1 %all-reduce.23.cloned.1.call-done = (bf16[96,768]{1,0:T(8,128)(2,1)}, bf16[96,3072]{1,0:T(8,128)(2,1)}, bf16[384,768]{1,0:T(8,128)(2,1)}) async-done(((bf16[96,768]{1,0:T(8,128)(2,1)}, bf16[96,3072]{1,0:T(8,128)(2,1)}, bf16[384,768]{1,0:T(8,128)(2,1)}), (bf16[96,768]{1,0:T(8,128)(2,1)}, bf16[96,3072]{1,0:T(8,128)(2,1)}, bf16[384,768]{1,0:T(8,128)(2,1)})) %all-reduce.23.cloned.1.call-update) | async-done | bytes 1327120 | tf_op jit(solution)/shard_map/psum | solution.py:298
  (372 shorter events, 310.3 us)
Async XLA Ops:
  7.2 58.4 %all-gather.8.cloned.1.call-start = ((), (), s32[]{:S(2)}) async-start(), calls=%async_computation.4 | async-start | bytes 3981312 | tf_op jit(solution)/shard_map/all_gather | solution.py:120
  7.9 148.7 %all-gather.10.cloned.1.call-start = ((), (), s32[]{:S(2)}) async-start(), calls=%async_computation.5 | async-start | bytes 1327104 | tf_op jit(solution)/shard_map/all_gather | solution.py:123
  8.7 153.3 %all-gather.12.cloned.1.call-start = ((), (), s32[]{:S(2)}) async-start(), calls=%async_computation.6 | async-start | bytes 5308416 | tf_op jit(solution)/shard_map/all_gather | solution.py:152
  9.4 172.3 %all-gather.14.cloned.1.call-start = ((), (), s32[]{:S(2)}) async-start(), calls=%async_computation.7 | async-start | bytes 5308416 | tf_op jit(solution)/shard_map/all_gather | solution.py:154
  10.0 435.2 %reduce-scatter.5.cloned.1.call-start = ((), (), s32[]{:S(2)}) async-start(), calls=%async_computation.8 | async-start | bytes 3981312 | tf_op jit(solution)/shard_map/reduce_scatter | solution.py:275
  10.2 61.7 %copy-start.3 = (bf16[12,1,1024,64]{2,3,1,0:T(8,128)(2,1)}, bf16[12,1,1024,64]{2,3,1,0:T(8,128)(2,1)S(1)}, u32[]{:S(2)}) copy-start(bf16[12,1,1024,64]{2,3,1,0:T(8,128)(2,1)S(1)} %fusion.104) | copy-start | bytes 4718596
  10.3 3.6 copy-start.31
  10.3 3.8 copy-start.32
  46.9 18.7 %copy-start.16 = (f32[768]{0:T(1024)}, f32[768]{0:T(1024)S(1)}, u32[]{:S(2)}) copy-start(f32[768]{0:T(1024)S(1)} %convert_element_type.236) | copy-start | bytes 9220
  46.9 18.7 %copy-start.21 = (f32[768]{0:T(1024)}, f32[768]{0:T(1024)S(1)}, u32[]{:S(2)}) copy-start(f32[768]{0:T(1024)S(1)} %convert_element_type.237) | copy-start | bytes 9220
  48.6 17.0 %copy-start = (bf16[1,1024,768]{1,2,0:T(8,128)(2,1)}, bf16[1,1024,768]{1,2,0:T(8,128)(2,1)S(1)}, u32[]{:S(2)}) copy-start(bf16[1,1024,768]{1,2,0:T(8,128)(2,1)S(1)} %copy.64) | copy-start | bytes 4718596
  48.6 4.1 copy-start.24
  48.9 23.0 %copy-start.14 = (f32[1024]{0:T(1024)}, f32[1024]{0:T(1024)S(1)}, u32[]{:S(2)}) copy-start(f32[1024]{0:T(1024)S(1)} %broadcast_multiply_fusion.5) | copy-start | bytes 12292
  49.4 22.5 %copy-start.18 = (f32[1024]{0:T(1024)}, f32[1024]{0:T(1024)S(1)}, u32[]{:S(2)}) copy-start(f32[1024]{0:T(1024)S(1)} %add_rsqrt_fusion.1) | copy-start | bytes 12292
  181.7 16.5 %copy-start.11 = (bf16[768,3072]{1,0:T(8,128)(2,1)S(1)}, bf16[768,3072]{1,0:T(8,128)(2,1)}, u32[]{:S(2)}) copy-start(bf16[768,3072]{1,0:T(8,128)(2,1)} %all-gather.12.cloned.1.call-done) | copy-start | bytes 14155780
  198.2 6.8 copy-start.34
  391.6 3.6 copy-start.1
  402.5 89.2 %reduce-scatter.7.cloned.1.call-start = ((), (), s32[]{:S(2)}) async-start(), calls=%async_computation.9 | async-start | bytes 1327104 | tf_op jit(solution)/shard_map/reduce_scatter | solution.py:284
  407.4 127.5 %reduce-scatter.9.cloned.1.call-start = ((), (), s32[]{:S(2)}) async-start(), calls=%async_computation.10 | async-start | bytes 5308416 | tf_op jit(solution)/shard_map/reduce_scatter | solution.py:204
  417.2 173.0 %reduce-scatter.11.cloned.1.call-start = ((), (), s32[]{:S(2)}) async-start(), calls=%async_computation.11 | async-start | bytes 5308416 | tf_op jit(solution)/shard_map/reduce_scatter | solution.py:210
  430.9 15.6 %copy-start.33 = (bf16[96]{0:T(256)(128)(2,1)S(1)}, bf16[96]{0:T(256)(128)(2,1)}, u32[]{:S(2)}) copy-start(bf16[96]{0:T(256)(128)(2,1)} %param.37) | copy-start | bytes 580
  431.0 195.7 %all-gather.16.cloned.1.call-start = ((), (), s32[]{:S(2)}) async-start(), calls=%async_computation.12 | async-start | bytes 2211840 | tf_op jit(solution)/shard_map/all_gather | solution.py:295
  445.2 238.4 %all-reduce.23.cloned.1.call-start = ((), (), s32[]{:S(2)}) async-start(), calls=%async_computation.13 | async-start | bytes 2654208 | tf_op jit(solution)/shard_map/psum | solution.py:298
  683.6 4.4 copy-start.13
  (43 other events, 94.5 us)
Sparse Core Ops, SparseCore 0:
  9.6 44.6 all-gather.7
  56.0 21.6 all-gather.9
  79.3 50.8 all-gather.11
  131.7 49.9 all-gather.13
  402.6 42.4 reduce-scatter.4
  447.9 31.5 reduce-scatter.6
  481.8 53.0 reduce-scatter.8
  537.2 53.0 reduce-scatter.10
  592.1 31.0 all-gather.15
  626.4 57.0 all-reduce.22
